TPU v7x, 32 devices: a whole 2x2x4 slice. The times are simulated.
32 devices in a mesh: dp: 8 (over z, x), tensor: 4 (over y, core).
Axes of the slice: x: 2, y: 2, z: 4, core: 2. Of those that a mesh axis runs over, the one named last changes fastest.
Arguments:
- tokens: bfloat16 [20480, 768], P(('dp', 'tensor')), may hold values from -6 to 6
- cotangent: bfloat16 [20480, 768], P(('dp', 'tensor')), may hold values from -6 to 6
- lengths: int32 [8, 8], P('dp'), may hold values from 1 to 512, 2048 in all within a row
- w_qkv: bfloat16 [768, 3, 768], P('dp', None, 'tensor'), may hold values from -0.21875 to 0.21875
- w_out: bfloat16 [768, 768], P('tensor', 'dp'), may hold values from -6 to 6
- w_fc: bfloat16 [768, 3072], P('dp', 'tensor'), may hold values from -0.21875 to 0.21875
- w_proj: bfloat16 [3072, 768], P('tensor', 'dp'), may hold values from -0.109375 to 0.109375
- ln1_gain: bfloat16 [768], P('dp'), may hold values from 0.25 to 1.75
- ln1_bias: bfloat16 [768], P('dp'), may hold values from -3 to 3
- ln2_gain: bfloat16 [768], P('dp'), may hold values from 0.25 to 1.75
- ln2_bias: bfloat16 [768], P('dp'), may hold values from -3 to 3
Outputs:
- block_out: bfloat16 [20480, 768], P(('dp', 'tensor'))
- input_grad: bfloat16 [20480, 768], P(('dp', 'tensor'))
- w_qkv_grad: float32 [768, 3, 768], P('dp', None, 'tensor')
- w_out_grad: float32 [768, 768], P('tensor', 'dp')
- w_fc_grad: float32 [768, 3072], P('dp', 'tensor')
- w_proj_grad: float32 [3072, 768], P('tensor', 'dp')
- ln1_gain_grad: float32 [768], P('dp')
- ln1_bias_grad: float32 [768], P('dp')
- ln2_gain_grad: float32 [768], P('dp')
- ln2_bias_grad: float32 [768], P('dp')
Inputs may be any that keep to these rules, and one draw needn't show every extreme that they name: `lengths`: row g lists the token counts of group g's 8 continuations in order after its 512-token prompt; each row sums to 2048 and its largest entry is exactly 512.
All inputs are finite; a program needn't handle non-finite values.
Results may differ from a plain program's by a relative error of at most 0.019.
The roundings to bfloat16 on the way count: a program that leaves them out, or rounds other values in their place, can miss the bound.
Values may be sent and summed in bfloat16 or wider, within the bound.
A program may use at most 192 MiB of HBM per device.

v0:
```python
import jax
import jax.numpy as jnp
from jax import lax
from jax.sharding import PartitionSpec as P

HEAD = 64
PROMPT = 512


def normalize(values):
    mean = jnp.mean(values, axis=-1, keepdims=True)
    centred = values - mean
    spread = jnp.mean(centred * centred, axis=-1, keepdims=True)
    factor = lax.rsqrt(spread + 1e-05)
    return (centred * factor, factor)


def norm_back(grad_out, normed, factor, gain):
    scaled = grad_out * gain
    first = jnp.mean(scaled, axis=-1, keepdims=True)
    second = jnp.mean(scaled * normed, axis=-1, keepdims=True)
    return factor * (scaled - first - normed * second)


def gelu_tanh(values):
    return jax.nn.gelu(values, approximate=True)


def inner_rows(left, right):
    return lax.dot_general(
        left, right, (((0,), (0,)), ((), ())), preferred_element_type=jnp.float32
    )


def times_trans(left, right):
    return lax.dot_general(
        left, right, (((1,), (1,)), ((), ())), preferred_element_type=jnp.float32
    )


def segment_ids(lengths, total):
    ends = PROMPT + jnp.cumsum(lengths[0])
    places = jnp.arange(total, dtype=jnp.int32)
    passed = jnp.sum((places[:, None] >= ends[None, :]).astype(jnp.int32), axis=1)
    return (places, jnp.where(places < PROMPT, -1, passed))


def visible(query_pos, query_seg, key_pos, key_seg):
    causal = key_pos[None, :] <= query_pos[:, None]
    shared = (key_seg[None, :] < 0) | (key_seg[None, :] == query_seg[:, None])
    return (causal & shared)[None]


def attend(queries, keys, values, places, segs, block, scale):
    count = queries.shape[0] // block

    def one(index):
        start = index * block
        query = lax.dynamic_slice_in_dim(queries, start, block, 0)
        mask = visible(
            lax.dynamic_slice_in_dim(places, start, block, 0),
            lax.dynamic_slice_in_dim(segs, start, block, 0),
            places,
            segs,
        )
        raw = jnp.einsum("qhd,khd->hqk", query, keys, preferred_element_type=jnp.float32) * scale
        magnitude = jnp.where(mask, jnp.abs(raw), -1e30)
        top = jnp.max(magnitude, axis=-1, keepdims=True)
        expo = jnp.where(mask, jnp.exp(magnitude - top), 0.0)
        total = jnp.sum(expo, axis=-1, keepdims=True)
        weights = (jnp.sign(raw) * (expo / total)).astype(jnp.bfloat16)
        mixed = jnp.einsum("hqk,khd->qhd", weights, values, preferred_element_type=jnp.float32)
        return (mixed.astype(jnp.bfloat16), (top + jnp.log(total))[..., 0])

    mixed, sums = lax.map(one, jnp.arange(count, dtype=jnp.int32))
    return (mixed.reshape(queries.shape[0], -1), sums)


def attend_back(queries, keys, values, grad_mixed, sums, places, segs, block, scale):
    count = queries.shape[0] // block

    def step(carry, inputs):
        key_grad, value_grad = carry
        index, lse_block = inputs
        start = index * block
        query = lax.dynamic_slice_in_dim(queries, start, block, 0)
        grad_block = lax.dynamic_slice_in_dim(grad_mixed, start, block, 0)
        mask = visible(
            lax.dynamic_slice_in_dim(places, start, block, 0),
            lax.dynamic_slice_in_dim(segs, start, block, 0),
            places,
            segs,
        )
        raw = jnp.einsum("qhd,khd->hqk", query, keys, preferred_element_type=jnp.float32) * scale
        prob = jnp.where(mask, jnp.exp(jnp.abs(raw) - lse_block[..., None]), 0.0)
        signed = jnp.sign(raw) * prob
        rounded = signed.astype(jnp.bfloat16)
        value_grad = value_grad + jnp.einsum(
            "hqk,qhd->khd", rounded, grad_block, preferred_element_type=jnp.float32
        )
        weight_grad = jnp.einsum(
            "qhd,khd->hqk", grad_block, values, preferred_element_type=jnp.float32
        )
        inner = jnp.sum(signed * weight_grad, axis=-1, keepdims=True)
        score_grad = (prob * weight_grad - signed * inner).astype(jnp.bfloat16)
        query_grad = (
            jnp.einsum("hqk,khd->qhd", score_grad, keys, preferred_element_type=jnp.float32) * scale
        )
        key_grad = (
            key_grad
            + jnp.einsum("hqk,qhd->khd", score_grad, query, preferred_element_type=jnp.float32)
            * scale
        )
        return ((key_grad, value_grad), query_grad)

    zeros = jnp.zeros(keys.shape, jnp.float32)
    (key_grad, value_grad), query_grad = lax.scan(
        step, (zeros, zeros), (jnp.arange(count, dtype=jnp.int32), sums)
    )
    return (query_grad.reshape(keys.shape), key_grad, value_grad)


def on_device(
    tokens, cotangent, lengths, w_qkv, w_out, w_fc, w_proj, ln1_gain, ln1_bias, ln2_gain, ln2_bias
):
    rows = tokens.shape[0]
    group = rows * lax.axis_size("tensor")
    block = group // max(1, group // 512)
    scale = HEAD ** (-0.5)
    pieces = (w_qkv, w_out, w_fc, w_proj, ln1_gain, ln1_bias, ln2_gain, ln2_bias)
    qkv_full, out_full, fc_full, proj_full, gain1, bias1, gain2, bias2 = (
        lax.all_gather(pieces[0], "dp", axis=0, tiled=True),
        lax.all_gather(pieces[1], "dp", axis=1, tiled=True),
        lax.all_gather(pieces[2], "dp", axis=0, tiled=True),
        lax.all_gather(pieces[3], "dp", axis=1, tiled=True),
        lax.all_gather(pieces[4], "dp", axis=0, tiled=True),
        lax.all_gather(pieces[5], "dp", axis=0, tiled=True),
        lax.all_gather(pieces[6], "dp", axis=0, tiled=True),
        lax.all_gather(pieces[7], "dp", axis=0, tiled=True),
    )
    gain1 = gain1.astype(jnp.float32)
    bias1 = bias1.astype(jnp.float32)
    gain2 = gain2.astype(jnp.float32)
    bias2 = bias2.astype(jnp.float32)
    width = qkv_full.shape[0]
    local = qkv_full.shape[2]
    heads = local // HEAD
    qkv_mat = qkv_full.reshape(width, 3 * local)
    places, segs = segment_ids(lengths, group)
    inputs = tokens.astype(jnp.float32)
    normed1, factor1 = normalize(inputs)
    lowered1 = (normed1 * gain1 + bias1).astype(jnp.bfloat16)
    all_norm1 = lax.all_gather(lowered1, "tensor", axis=0, tiled=True)
    projected = jnp.dot(all_norm1, qkv_mat, preferred_element_type=jnp.float32).astype(jnp.bfloat16)
    projected = projected.reshape(group, 3, heads, HEAD)
    queries = projected[:, 0]
    keys = projected[:, 1]
    values = projected[:, 2]
    mixed, sums = attend(queries, keys, values, places, segs, block, scale)
    part = mixed
    resid = inputs + lax.psum_scatter(
        jnp.dot(part, out_full, preferred_element_type=jnp.float32).astype(jnp.bfloat16),
        "tensor",
        scatter_dimension=0,
        tiled=True,
    ).astype(jnp.float32)
    normed2, factor2 = normalize(resid)
    lowered2 = (normed2 * gain2 + bias2).astype(jnp.bfloat16)
    all_norm2 = lax.all_gather(lowered2, "tensor", axis=0, tiled=True)
    hidden_pre = jnp.dot(all_norm2, fc_full, preferred_element_type=jnp.float32)
    hidden, gelu_pull = jax.vjp(gelu_tanh, hidden_pre)
    hidden_low = hidden.astype(jnp.bfloat16)
    part = hidden_low
    mlp_rows = lax.psum_scatter(
        jnp.dot(part, proj_full, preferred_element_type=jnp.float32).astype(jnp.bfloat16),
        "tensor",
        scatter_dimension=0,
        tiled=True,
    ).astype(jnp.float32)
    block_out = (resid + mlp_rows).astype(jnp.bfloat16)
    grad_all = lax.all_gather(cotangent, "tensor", axis=0, tiled=True)
    hidden_grad = times_trans(grad_all, proj_full)
    proj_grad = inner_rows(hidden_low, grad_all)
    pre_low = gelu_pull(hidden_grad)[0].astype(jnp.bfloat16)
    fc_grad = inner_rows(all_norm2, pre_low)
    part = pre_low
    norm2_grad = lax.psum_scatter(
        times_trans(part, fc_full).astype(jnp.bfloat16), "tensor", scatter_dimension=0, tiled=True
    ).astype(jnp.float32)
    gain2_part = jnp.sum(norm2_grad * normed2, axis=0)
    bias2_part = jnp.sum(norm2_grad, axis=0)
    resid_grad = cotangent.astype(jnp.float32) + norm_back(norm2_grad, normed2, factor2, gain2)
    resid_low = resid_grad.astype(jnp.bfloat16)
    resid_all = lax.all_gather(resid_low, "tensor", axis=0, tiled=True)
    out_grad = inner_rows(mixed, resid_all)
    mixed_grad = times_trans(resid_all, out_full).astype(jnp.bfloat16).reshape(group, heads, HEAD)
    query_grad, key_grad, value_grad = attend_back(
        queries, keys, values, mixed_grad, sums, places, segs, block, scale
    )
    qkv_grad_low = (
        jnp.stack([query_grad, key_grad, value_grad], axis=1)
        .astype(jnp.bfloat16)
        .reshape(group, 3 * local)
    )
    qkv_grad = inner_rows(all_norm1, qkv_grad_low).reshape(width, 3, local)
    part = qkv_grad_low
    norm1_grad = lax.psum_scatter(
        times_trans(part, qkv_mat).astype(jnp.bfloat16), "tensor", scatter_dimension=0, tiled=True
    ).astype(jnp.float32)
    gain1_part = jnp.sum(norm1_grad * normed1, axis=0)
    bias1_part = jnp.sum(norm1_grad, axis=0)
    input_grad = (resid_grad + norm_back(norm1_grad, normed1, factor1, gain1)).astype(jnp.bfloat16)
    qkv_sum, out_sum, fc_sum, proj_sum, gain1_share, bias1_share, gain2_share, bias2_share = (
        lax.psum_scatter(qkv_grad, "dp", scatter_dimension=0, tiled=True),
        lax.psum_scatter(out_grad, "dp", scatter_dimension=1, tiled=True),
        lax.psum_scatter(fc_grad, "dp", scatter_dimension=0, tiled=True),
        lax.psum_scatter(proj_grad, "dp", scatter_dimension=1, tiled=True),
        lax.psum_scatter(gain1_part, "dp", scatter_dimension=0, tiled=True),
        lax.psum_scatter(bias1_part, "dp", scatter_dimension=0, tiled=True),
        lax.psum_scatter(gain2_part, "dp", scatter_dimension=0, tiled=True),
        lax.psum_scatter(bias2_part, "dp", scatter_dimension=0, tiled=True),
    )
    gain1_sum, bias1_sum, gain2_sum, bias2_sum = lax.psum(
        (gain1_share, bias1_share, gain2_share, bias2_share), "tensor"
    )
    return (
        block_out,
        input_grad,
        qkv_sum,
        out_sum,
        fc_sum,
        proj_sum,
        gain1_sum,
        bias1_sum,
        gain2_sum,
        bias2_sum,
    )


def solution(mesh):
    placed = (
        P(("dp", "tensor"), None),
        P(("dp", "tensor"), None),
        P("dp", None),
        P("dp", None, "tensor"),
        P("tensor", "dp"),
        P("dp", "tensor"),
        P("tensor", "dp"),
        P("dp"),
        P("dp"),
        P("dp"),
        P("dp"),
    )
    return jax.shard_map(
        on_device,
        mesh=mesh,
        in_specs=placed,
        out_specs=(
            P(("dp", "tensor"), None),
            P(("dp", "tensor"), None),
            P("dp", None, "tensor"),
            P("tensor", "dp"),
            P("dp", "tensor"),
            P("tensor", "dp"),
            P("dp"),
            P("dp"),
            P("dp"),
            P("dp"),
        ),
        check_vma=False,
    )
```

profile of v0, /device:TPU:0, one launch (start us, length us, event | category | flops | bytes accessed | tf_op | source)
XLA Modules:
  0.0 1164.4 jit_solution(4583404668944278764)
XLA Ops:
  13.4 23.9 %all-reduce.10 = (bf16[768]{0:T(1024)(128)(2,1)}, bf16[768]{0:T(1024)(128)(2,1)}, bf16[768]{0:T(1024)(128)(2,1)S(1)}, bf16[768]{0:T(1024)(128)(2,1)S(1)}) all-reduce(bf16[768]{0:T(1024)(128)(2,1)S(1)} %dynamic-update-slice.3, bf16[768]{0:T(1024)(128)(2,1)S(1)} %dynamic-update-slice.2, ...), channel_id=1, replica_groups=mesh['dp'=8,'tensor'=4] {'dp'}, use_global_device_ids=true, to_apply=%add.3 | all-reduce | flops 3072 | bytes 12288
  43.6 35.5 %all_gather.39 = bf16[768,3,192]{2,1,0:T(4,128)(2,1)S(1)} all-gather(bf16[96,3,192]{2,1,0:T(4,128)(2,1)S(1)} %copy.32), channel_id=1, replica_groups=mesh['dp'=8,'tensor'=4] {'dp'}, dimensions={0}, use_global_device_ids=true | all-gather | bytes 995328 | tf_op jit(solution)/shard_map/all_gather | solution.py:132
  80.1 33.6 %all_gather.40 = bf16[192,768]{0,1:T(8,128)(2,1)} all-gather(bf16[192,96]{0,1:T(8,128)(2,1)S(1)} %copy.35), channel_id=1, replica_groups=mesh['dp'=8,'tensor'=4] {'dp'}, dimensions={1}, use_global_device_ids=true | all-gather | bytes 331776 | tf_op jit(solution)/shard_map/all_gather | solution.py:133
  119.7 122.1 %while.29 = (s32[]{:T(128)}, bf16[5,512,3,64]{1,3,2,0:T(8,128)(2,1)S(1)}, f32[5,3,512]{2,1,0:T(4,128)S(1)}, s32[5]{0:T(128)S(1)}, bf16[2560,3,64]{0,2,1:T(8,128)...) while((s32[]{:T(128)}, ...), condition=%wide.region_7.8_spmd.clone, body=%wide.region_4.7_spmd.clone.sunk | while | flops 1086686208 | bytes 54895824 | solution.py:75
  128.0 5.5 fusion.126
  133.5 10.6 fusion.127
  157.8 10.6 fusion.127
  182.2 10.6 fusion.127
  206.6 10.6 fusion.127
  231.0 10.6 fusion.127
  248.8 40.7 %reduce-scatter.11.cloned.1.call-done = bf16[640,768]{1,0:T(8,128)(2,1)} async-done(((bf16[2560,768]{1,0:T(8,128)(2,1)}), bf16[640,768]{1,0:T(8,128)(2,1)}) %reduce-scatter.11.cloned.1.call-update) | async-done | bytes 983056 | tf_op jit(solution)/shard_map/reduce_scatter | solution.py:161
  294.4 28.8 %all-gather.15.cloned.1.call-done = bf16[2560,768]{1,0:T(8,128)(2,1)} async-done(((bf16[640,768]{1,0:T(8,128)(2,1)}), bf16[2560,768]{1,0:T(8,128)(2,1)}) %all-gather.15.cloned.1.call-update) | async-done | bytes 3932176 | tf_op jit(solution)/shard_map/all_gather | solution.py:181
  323.2 8.8 fusion.75
  332.1 34.7 %all-gather.11.cloned.1.call-done = bf16[768,768]{1,0:T(8,128)(2,1)} async-done(((bf16[96,768]{1,0:T(8,128)(2,1)}), bf16[768,768]{1,0:T(8,128)(2,1)}) %all-gather.11.cloned.1.call-update) | async-done | bytes 1179664 | tf_op jit(solution)/shard_map/all_gather | solution.py:134
  366.7 33.4 %all-gather.9.cloned.1.call-done = bf16[2560,768]{1,0:T(8,128)(2,1)} async-done(((bf16[640,768]{1,0:T(8,128)(2,1)}), bf16[2560,768]{1,0:T(8,128)(2,1)}) %all-gather.9.cloned.1.call-update) | async-done | bytes 3932176 | tf_op jit(solution)/shard_map/all_gather | solution.py:169
  400.1 13.6 %fusion.43 = (bf16[2560,768]{1,0:T(8,128)(2,1)S(1)}, f32[2560,768]{1,0:T(8,128)}) fusion(f32[2560,768]{1,0:T(8,128)} %fusion.75, bf16[2560,768]{1,0:T(8,128)(2,1)} %all-gather.9.cloned.1.call-done, bf16[768,768]{1,0:T(8,128)(2,1)} %all-gather.11.cloned.1.call-done), kind=kOutput, calls=%fused_computation.55 | convolution fusion | flops 3059220480 | bytes 24772608 | tf_op jit(solution)/shard_map/dot_general | solution.py:170
  421.0 42.6 %reduce-scatter.15.cloned.1.call-done = bf16[640,768]{1,0:T(8,128)(2,1)} async-done(((bf16[2560,768]{1,0:T(8,128)(2,1)}), bf16[640,768]{1,0:T(8,128)(2,1)}) %reduce-scatter.15.cloned.1.call-update) | async-done | bytes 983056 | tf_op jit(solution)/shard_map/reduce_scatter | solution.py:187
  470.5 32.9 %all-gather.17.cloned.1.call-done = bf16[2560,768]{1,0:T(8,128)(2,1)} async-done(((bf16[640,768]{1,0:T(8,128)(2,1)}), bf16[2560,768]{1,0:T(8,128)(2,1)}) %all-gather.17.cloned.1.call-update) | async-done | bytes 3932176 | tf_op jit(solution)/shard_map/all_gather | solution.py:194
  512.9 323.7 %while.30 = (s32[]{:T(128)}, f32[2560,3,64]{0,2,1:T(8,128)}, f32[2560,3,64]{0,2,1:T(8,128)}, bf16[5,512,3,64]{1,0,3,2:T(8,128)(2,1)}, s32[5]{0:T(128)S(1)}, /*in...) while((s32[]{:T(128)}, f32[2560,3,64]{0,2,1:T(8,128)}, ...), condition=%wide.region_17.18_spmd.clone.clone, body=%wide.region_15.17_spmd.clone.clone.sunk | while | flops 2622784512 | bytes 218457456 | solution.py:117
  519.5 12.2 %fusion.139 = f32[2560,3,64]{0,2,1:T(8,128)} fusion(f32[3,512,2560]{2,1,0:T(8,128)S(1)} %fusion.137, f32[3,512]{1,0:T(4,128)S(1)} %dynamic-slice_bitcast_fusion.2, pred[512,2560]{1,0:T(8,128)(4,1)S(1)} %or_and_fusion.5, f32[2560,3,64]{0,2,1:T(8,128)} %get-tuple-element.492, pred[]{:T(512)S(6)} %compare.3, ...), kind=kOutput, calls=%fused_computation.30.clone.1 | convolution fusion | flops 531824640 | bytes 21174276 | tf_op jit(solution)/shard_map/while/body/eval_jaxpr/hqk,qhd->khd/dot_general | solution.py:98
  531.7 15.0 %multiply_reduce_fusion.3 = (f32[3,512]{1,0:T(4,128)S(1)}, f32[3,512,2560]{2,1,0:T(8,128)}) fusion(f32[3,512,2560]{2,1,0:T(8,128)S(1)} %fusion.137, f32[3,512]{1,0:T(4,128)S(1)} %dynamic-slice_bitcast_fusion.2, pred[512,2560]{1,0:T(8,128)(4,1)S(1)} %or_and_fusion.5, bf16[2560,3,64]{0,2,1:T(8,128)(2,1)S(1)} %copy-done.12, ...), kind=kOutput, calls=%fused_computation.19.clone.1 | convolution fusion | flops 534772224 | bytes 33959940 | tf_op jit(solution)/shard_map/while/body/eval_jaxpr/qhd,khd->hqk/dot_general | solution.py:101
  546.7 15.2 %subtract_convert_fusion.2 = bf16[3,512,2560]{2,1,0:T(8,128)(2,1)S(1)} fusion(f32[3,512,2560]{2,1,0:T(8,128)} %get-tuple-element.433, f32[3,512,2560]{2,1,0:T(8,128)} %copy-done, f32[3,512]{1,0:T(4,128)S(1)} %get-tuple-element.434, f32[3,512]{1,0:T(4,128)S(1)} %dynamic-slice_bitcast_fusion.2, pred[512,2560]{1,0:T(8,128)(4,1)S(1)} %or_and_fusion.5), kind=kLoop, calls=%fused_computation.18.clone.1 | loop fusion | flops 39321600 | bytes 40644608 | tf_op jit(solution)/shard_map/while/body/eval_jaxpr/convert_element_type | solution.py:105
  567.3 8.7 dynamic_update_slice.23
  582.4 14.4 %fusion.139 = f32[2560,3,64]{0,2,1:T(8,128)} fusion(f32[3,512,2560]{2,1,0:T(8,128)S(1)} %fusion.137, f32[3,512]{1,0:T(4,128)S(1)} %dynamic-slice_bitcast_fusion.2, pred[512,2560]{1,0:T(8,128)(4,1)S(1)} %or_and_fusion.5, f32[2560,3,64]{0,2,1:T(8,128)} %get-tuple-element.492, pred[]{:T(512)S(6)} %compare.3, ...), kind=kOutput, calls=%fused_computation.30.clone.1 | convolution fusion | flops 531824640 | bytes 21174276 | tf_op jit(solution)/shard_map/while/body/eval_jaxpr/hqk,qhd->khd/dot_general | solution.py:98
  596.8 15.0 %multiply_reduce_fusion.3 = (f32[3,512]{1,0:T(4,128)S(1)}, f32[3,512,2560]{2,1,0:T(8,128)}) fusion(f32[3,512,2560]{2,1,0:T(8,128)S(1)} %fusion.137, f32[3,512]{1,0:T(4,128)S(1)} %dynamic-slice_bitcast_fusion.2, pred[512,2560]{1,0:T(8,128)(4,1)S(1)} %or_and_fusion.5, bf16[2560,3,64]{0,2,1:T(8,128)(2,1)S(1)} %copy-done.12, ...), kind=kOutput, calls=%fused_computation.19.clone.1 | convolution fusion | flops 534772224 | bytes 33959940 | tf_op jit(solution)/shard_map/while/body/eval_jaxpr/qhd,khd->hqk/dot_general | solution.py:101
  611.8 15.2 %subtract_convert_fusion.2 = bf16[3,512,2560]{2,1,0:T(8,128)(2,1)S(1)} fusion(f32[3,512,2560]{2,1,0:T(8,128)} %get-tuple-element.433, f32[3,512,2560]{2,1,0:T(8,128)} %copy-done, f32[3,512]{1,0:T(4,128)S(1)} %get-tuple-element.434, f32[3,512]{1,0:T(4,128)S(1)} %dynamic-slice_bitcast_fusion.2, pred[512,2560]{1,0:T(8,128)(4,1)S(1)} %or_and_fusion.5), kind=kLoop, calls=%fused_computation.18.clone.1 | loop fusion | flops 39321600 | bytes 40644608 | tf_op jit(solution)/shard_map/while/body/eval_jaxpr/convert_element_type | solution.py:105
  632.3 8.7 dynamic_update_slice.23
  647.4 14.4 %fusion.139 = f32[2560,3,64]{0,2,1:T(8,128)} fusion(f32[3,512,2560]{2,1,0:T(8,128)S(1)} %fusion.137, f32[3,512]{1,0:T(4,128)S(1)} %dynamic-slice_bitcast_fusion.2, pred[512,2560]{1,0:T(8,128)(4,1)S(1)} %or_and_fusion.5, f32[2560,3,64]{0,2,1:T(8,128)} %get-tuple-element.492, pred[]{:T(512)S(6)} %compare.3, ...), kind=kOutput, calls=%fused_computation.30.clone.1 | convolution fusion | flops 531824640 | bytes 21174276 | tf_op jit(solution)/shard_map/while/body/eval_jaxpr/hqk,qhd->khd/dot_general | solution.py:98
  661.8 15.0 %multiply_reduce_fusion.3 = (f32[3,512]{1,0:T(4,128)S(1)}, f32[3,512,2560]{2,1,0:T(8,128)}) fusion(f32[3,512,2560]{2,1,0:T(8,128)S(1)} %fusion.137, f32[3,512]{1,0:T(4,128)S(1)} %dynamic-slice_bitcast_fusion.2, pred[512,2560]{1,0:T(8,128)(4,1)S(1)} %or_and_fusion.5, bf16[2560,3,64]{0,2,1:T(8,128)(2,1)S(1)} %copy-done.12, ...), kind=kOutput, calls=%fused_computation.19.clone.1 | convolution fusion | flops 534772224 | bytes 33959940 | tf_op jit(solution)/shard_map/while/body/eval_jaxpr/qhd,khd->hqk/dot_general | solution.py:101
  676.8 15.2 %subtract_convert_fusion.2 = bf16[3,512,2560]{2,1,0:T(8,128)(2,1)S(1)} fusion(f32[3,512,2560]{2,1,0:T(8,128)} %get-tuple-element.433, f32[3,512,2560]{2,1,0:T(8,128)} %copy-done, f32[3,512]{1,0:T(4,128)S(1)} %get-tuple-element.434, f32[3,512]{1,0:T(4,128)S(1)} %dynamic-slice_bitcast_fusion.2, pred[512,2560]{1,0:T(8,128)(4,1)S(1)} %or_and_fusion.5), kind=kLoop, calls=%fused_computation.18.clone.1 | loop fusion | flops 39321600 | bytes 40644608 | tf_op jit(solution)/shard_map/while/body/eval_jaxpr/convert_element_type | solution.py:105
  697.4 8.7 dynamic_update_slice.23
  712.5 14.4 %fusion.139 = f32[2560,3,64]{0,2,1:T(8,128)} fusion(f32[3,512,2560]{2,1,0:T(8,128)S(1)} %fusion.137, f32[3,512]{1,0:T(4,128)S(1)} %dynamic-slice_bitcast_fusion.2, pred[512,2560]{1,0:T(8,128)(4,1)S(1)} %or_and_fusion.5, f32[2560,3,64]{0,2,1:T(8,128)} %get-tuple-element.492, pred[]{:T(512)S(6)} %compare.3, ...), kind=kOutput, calls=%fused_computation.30.clone.1 | convolution fusion | flops 531824640 | bytes 21174276 | tf_op jit(solution)/shard_map/while/body/eval_jaxpr/hqk,qhd->khd/dot_general | solution.py:98
  726.9 15.0 %multiply_reduce_fusion.3 = (f32[3,512]{1,0:T(4,128)S(1)}, f32[3,512,2560]{2,1,0:T(8,128)}) fusion(f32[3,512,2560]{2,1,0:T(8,128)S(1)} %fusion.137, f32[3,512]{1,0:T(4,128)S(1)} %dynamic-slice_bitcast_fusion.2, pred[512,2560]{1,0:T(8,128)(4,1)S(1)} %or_and_fusion.5, bf16[2560,3,64]{0,2,1:T(8,128)(2,1)S(1)} %copy-done.12, ...), kind=kOutput, calls=%fused_computation.19.clone.1 | convolution fusion | flops 534772224 | bytes 33959940 | tf_op jit(solution)/shard_map/while/body/eval_jaxpr/qhd,khd->hqk/dot_general | solution.py:101
  741.9 15.2 %subtract_convert_fusion.2 = bf16[3,512,2560]{2,1,0:T(8,128)(2,1)S(1)} fusion(f32[3,512,2560]{2,1,0:T(8,128)} %get-tuple-element.433, f32[3,512,2560]{2,1,0:T(8,128)} %copy-done, f32[3,512]{1,0:T(4,128)S(1)} %get-tuple-element.434, f32[3,512]{1,0:T(4,128)S(1)} %dynamic-slice_bitcast_fusion.2, pred[512,2560]{1,0:T(8,128)(4,1)S(1)} %or_and_fusion.5), kind=kLoop, calls=%fused_computation.18.clone.1 | loop fusion | flops 39321600 | bytes 40644608 | tf_op jit(solution)/shard_map/while/body/eval_jaxpr/convert_element_type | solution.py:105
  762.5 8.7 dynamic_update_slice.23
  777.6 14.4 %fusion.139 = f32[2560,3,64]{0,2,1:T(8,128)} fusion(f32[3,512,2560]{2,1,0:T(8,128)S(1)} %fusion.137, f32[3,512]{1,0:T(4,128)S(1)} %dynamic-slice_bitcast_fusion.2, pred[512,2560]{1,0:T(8,128)(4,1)S(1)} %or_and_fusion.5, f32[2560,3,64]{0,2,1:T(8,128)} %get-tuple-element.492, pred[]{:T(512)S(6)} %compare.3, ...), kind=kOutput, calls=%fused_computation.30.clone.1 | convolution fusion | flops 531824640 | bytes 21174276 | tf_op jit(solution)/shard_map/while/body/eval_jaxpr/hqk,qhd->khd/dot_general | solution.py:98
  792.0 15.0 %multiply_reduce_fusion.3 = (f32[3,512]{1,0:T(4,128)S(1)}, f32[3,512,2560]{2,1,0:T(8,128)}) fusion(f32[3,512,2560]{2,1,0:T(8,128)S(1)} %fusion.137, f32[3,512]{1,0:T(4,128)S(1)} %dynamic-slice_bitcast_fusion.2, pred[512,2560]{1,0:T(8,128)(4,1)S(1)} %or_and_fusion.5, bf16[2560,3,64]{0,2,1:T(8,128)(2,1)S(1)} %copy-done.12, ...), kind=kOutput, calls=%fused_computation.19.clone.1 | convolution fusion | flops 534772224 | bytes 33959940 | tf_op jit(solution)/shard_map/while/body/eval_jaxpr/qhd,khd->hqk/dot_general | solution.py:101
  807.0 15.2 %subtract_convert_fusion.2 = bf16[3,512,2560]{2,1,0:T(8,128)(2,1)S(1)} fusion(f32[3,512,2560]{2,1,0:T(8,128)} %get-tuple-element.433, f32[3,512,2560]{2,1,0:T(8,128)} %copy-done, f32[3,512]{1,0:T(4,128)S(1)} %get-tuple-element.434, f32[3,512]{1,0:T(4,128)S(1)} %dynamic-slice_bitcast_fusion.2, pred[512,2560]{1,0:T(8,128)(4,1)S(1)} %or_and_fusion.5), kind=kLoop, calls=%fused_computation.18.clone.1 | loop fusion | flops 39321600 | bytes 40644608 | tf_op jit(solution)/shard_map/while/body/eval_jaxpr/convert_element_type | solution.py:105
  827.5 8.7 dynamic_update_slice.23
  849.9 9.9 convolution_convert_fusion.1
  859.9 8.1 fusion.76
  868.2 9.6 fusion.73
  877.9 7.7 fusion.44
  893.8 37.1 %all-reduce.8 = (f32[768]{0:T(1024)S(1)}, f32[768]{0:T(1024)S(1)}, f32[768]{0:T(1024)S(1)}, f32[768]{0:T(1024)S(1)}) all-reduce(f32[768]{0:T(1024)S(1)} %get-tuple-element.224, f32[768]{0:T(1024)S(1)} %get-tuple-element.229, f32[768]{0:T(1024)S(1)} %copy-done.34, ...), channel_id=10, replica_groups=mesh['dp'=8,'tensor'=4] {'dp'}, use_global_device_ids=true, to_apply=%region_26.27.clone | all-reduce | flops 3072 | bytes 24576
  931.2 6.4 all-reduce.9
  941.8 68.8 %reduce-scatter.21.cloned.1.call-done = f32[96,768]{1,0:T(8,128)} async-done(((f32[768,768]{1,0:T(8,128)}), f32[96,768]{1,0:T(8,128)}) %reduce-scatter.21.cloned.1.call-update) | async-done | bytes 294928 | tf_op jit(solution)/shard_map/reduce_scatter | solution.py:216
  1010.6 73.1 %reduce-scatter.23.cloned.1.call-done = f32[768,96]{0,1:T(8,128)} async-done(((f32[768,768]{0,1:T(8,128)}), f32[768,96]{0,1:T(8,128)}) %reduce-scatter.23.cloned.1.call-update) | async-done | bytes 294928 | tf_op jit(solution)/shard_map/reduce_scatter | solution.py:217
  1083.8 73.1 %reduce-scatter.19.cloned.1.call-done = f32[96,3,192]{2,0,1:T(8,128)} async-done(((f32[768,3,192]{2,0,1:T(8,128)}), f32[96,3,192]{2,0,1:T(8,128)}) %reduce-scatter.19.cloned.1.call-update) | async-done | bytes 221200 | tf_op jit(solution)/shard_map/reduce_scatter | solution.py:214
  (300 shorter events, 193.6 us)
Async XLA Ops:
  8.0 35.1 %copy-start.40 = (s32[1,8]{1,0:T(1,128)S(1)}, s32[1,8]{1,0:T(1,128)}, u32[]{:S(2)}) copy-start(s32[1,8]{1,0:T(1,128)} %param.17) | copy-start | bytes 100
  8.0 35.3 %copy-start.29 = (bf16[192,96]{1,0:T(8,128)(2,1)S(1)}, bf16[192,96]{1,0:T(8,128)(2,1)}, u32[]{:S(2)}) copy-start(bf16[192,96]{1,0:T(8,128)(2,1)} %param.19) | copy-start | bytes 110596
  8.0 35.4 %copy-start.16 = (bf16[96,3,192]{2,0,1:T(8,128)(2,1)S(1)}, bf16[96,3,192]{2,0,1:T(8,128)(2,1)}, u32[]{:S(2)}) copy-start(bf16[96,3,192]{2,0,1:T(8,128)(2,1)} %param.18) | copy-start | bytes 331780
  8.0 105.7 %all-gather.7.cloned.1.call-start = ((), (), s32[]{:S(2)}) async-start(), calls=%async_computation.8 | async-start | bytes 4915200 | tf_op jit(solution)/shard_map/all_gather | solution.py:153
  43.0 246.5 %reduce-scatter.11.cloned.1.call-start = ((), (), s32[]{:S(2)}) async-start(), calls=%async_computation.9 | async-start | bytes 4915200 | tf_op jit(solution)/shard_map/reduce_scatter | solution.py:161
  80.0 38.3 %copy-start.14 = (bf16[768,3,192]{0,2,1:T(8,128)(2,1)}, bf16[768,3,192]{0,2,1:T(8,128)(2,1)S(1)}, u32[]{:S(2)}) copy-start(bf16[768,3,192]{0,2,1:T(8,128)(2,1)S(1)} %copy.33) | copy-start | bytes 2654212
  246.9 42.6 %copy-start.1 = (bf16[640,768]{1,0:T(8,128)(2,1)S(1)}, bf16[640,768]{1,0:T(8,128)(2,1)}, u32[]{:S(2)}) copy-start(bf16[640,768]{1,0:T(8,128)(2,1)} %param.15) | copy-start | bytes 2949124
  247.0 47.5 %all-gather.13.cloned.1.call-start = ((), (), s32[]{:S(2)}) async-start(), calls=%async_computation.12 | async-start | bytes 1327104 | tf_op jit(solution)/shard_map/all_gather | solution.py:135
  247.5 75.7 %all-gather.15.cloned.1.call-start = ((), (), s32[]{:S(2)}) async-start(), calls=%async_computation.14 | async-start | bytes 4915200 | tf_op jit(solution)/shard_map/all_gather | solution.py:181
  248.1 118.6 %all-gather.11.cloned.1.call-start = ((), (), s32[]{:S(2)}) async-start(), calls=%async_computation.11 | async-start | bytes 1327104 | tf_op jit(solution)/shard_map/all_gather | solution.py:134
  248.7 151.4 %all-gather.9.cloned.1.call-start = ((), (), s32[]{:S(2)}) async-start(), calls=%async_computation.10 | async-start | bytes 4915200 | tf_op jit(solution)/shard_map/all_gather | solution.py:169
  248.8 217.6 %copy-start.21 = (f32[768]{0:T(1024)}, f32[768]{0:T(1024)S(1)}, u32[]{:S(2)}) copy-start(f32[768]{0:T(1024)S(1)} %convert_element_type.109) | copy-start | bytes 9220
  291.2 175.2 %copy-start.17 = (f32[640]{0:T(1024)}, f32[640]{0:T(1024)S(1)}, u32[]{:S(2)}) copy-start(f32[640]{0:T(1024)S(1)} %broadcast_multiply_fusion.4) | copy-start | bytes 7684
  292.9 173.5 %copy-start.23 = (f32[640]{0:T(1024)}, f32[640]{0:T(1024)S(1)}, u32[]{:S(2)}) copy-start(f32[640]{0:T(1024)S(1)} %add_rsqrt_fusion) | copy-start | bytes 7684
  294.4 169.2 %reduce-scatter.15.cloned.1.call-start = ((), (), s32[]{:S(2)}) async-start(), calls=%async_computation.15 | async-start | bytes 4915200 | tf_op jit(solution)/shard_map/reduce_scatter | solution.py:187
  400.1 15.6 %copy-start.39 = (bf16[768,768]{1,0:T(8,128)(2,1)S(1)}, bf16[768,768]{1,0:T(8,128)(2,1)}, u32[]{:S(2)}) copy-start(bf16[768,768]{1,0:T(8,128)(2,1)} %all-gather.11.cloned.1.call-done) | copy-start | bytes 3538948
  420.5 82.9 %all-gather.17.cloned.1.call-start = ((), (), s32[]{:S(2)}) async-start(), calls=%async_computation.16 | async-start | bytes 4915200 | tf_op jit(solution)/shard_map/all_gather | solution.py:194
  470.4 416.2 %reduce-scatter.25.cloned.1.call-start = ((), (), s32[]{:S(2)}) async-start(), calls=%async_computation.21 | async-start | bytes 884736
  508.3 383.3 %reduce-scatter.17.cloned.1.call-start = ((), (), s32[]{:S(2)}) async-start(), calls=%async_computation.17 | async-start | bytes 4915200 | tf_op jit(solution)/shard_map/reduce_scatter | solution.py:207
  519.5 12.2 %copy-start = (f32[3,512,2560]{2,1,0:T(8,128)}, f32[3,512,2560]{2,1,0:T(8,128)S(1)}, u32[]{:S(2)}) copy-start(f32[3,512,2560]{2,1,0:T(8,128)S(1)} %fusion.137) | copy-start | bytes 47185924 | tf_op jit(solution)/shard_map/while
  519.5 12.2 %copy-start.12 = (bf16[2560,3,64]{0,2,1:T(8,128)(2,1)S(1)}, bf16[2560,3,64]{0,2,1:T(8,128)(2,1)}, u32[]{:S(2)}) copy-start(bf16[2560,3,64]{0,2,1:T(8,128)(2,1)} %get-tuple-element.517) | copy-start | bytes 2949124 | tf_op jit(solution)/shard_map/while
  567.0 9.0 copy-start.4
  582.4 14.4 %copy-start = (f32[3,512,2560]{2,1,0:T(8,128)}, f32[3,512,2560]{2,1,0:T(8,128)S(1)}, u32[]{:S(2)}) copy-start(f32[3,512,2560]{2,1,0:T(8,128)S(1)} %fusion.137) | copy-start | bytes 47185924 | tf_op jit(solution)/shard_map/while
  582.4 14.4 %copy-start.12 = (bf16[2560,3,64]{0,2,1:T(8,128)(2,1)S(1)}, bf16[2560,3,64]{0,2,1:T(8,128)(2,1)}, u32[]{:S(2)}) copy-start(bf16[2560,3,64]{0,2,1:T(8,128)(2,1)} %get-tuple-element.517) | copy-start | bytes 2949124 | tf_op jit(solution)/shard_map/while
  632.0 9.0 copy-start.4
  647.4 14.4 %copy-start = (f32[3,512,2560]{2,1,0:T(8,128)}, f32[3,512,2560]{2,1,0:T(8,128)S(1)}, u32[]{:S(2)}) copy-start(f32[3,512,2560]{2,1,0:T(8,128)S(1)} %fusion.137) | copy-start | bytes 47185924 | tf_op jit(solution)/shard_map/while
  647.4 14.4 %copy-start.12 = (bf16[2560,3,64]{0,2,1:T(8,128)(2,1)S(1)}, bf16[2560,3,64]{0,2,1:T(8,128)(2,1)}, u32[]{:S(2)}) copy-start(bf16[2560,3,64]{0,2,1:T(8,128)(2,1)} %get-tuple-element.517) | copy-start | bytes 2949124 | tf_op jit(solution)/shard_map/while
  697.1 9.0 copy-start.4
  712.5 14.4 %copy-start = (f32[3,512,2560]{2,1,0:T(8,128)}, f32[3,512,2560]{2,1,0:T(8,128)S(1)}, u32[]{:S(2)}) copy-start(f32[3,512,2560]{2,1,0:T(8,128)S(1)} %fusion.137) | copy-start | bytes 47185924 | tf_op jit(solution)/shard_map/while
  712.5 14.4 %copy-start.12 = (bf16[2560,3,64]{0,2,1:T(8,128)(2,1)S(1)}, bf16[2560,3,64]{0,2,1:T(8,128)(2,1)}, u32[]{:S(2)}) copy-start(bf16[2560,3,64]{0,2,1:T(8,128)(2,1)} %get-tuple-element.517) | copy-start | bytes 2949124 | tf_op jit(solution)/shard_map/while
  762.2 9.0 copy-start.4
  777.6 14.4 %copy-start = (f32[3,512,2560]{2,1,0:T(8,128)}, f32[3,512,2560]{2,1,0:T(8,128)S(1)}, u32[]{:S(2)}) copy-start(f32[3,512,2560]{2,1,0:T(8,128)S(1)} %fusion.137) | copy-start | bytes 47185924 | tf_op jit(solution)/shard_map/while
  777.6 14.4 %copy-start.12 = (bf16[2560,3,64]{0,2,1:T(8,128)(2,1)S(1)}, bf16[2560,3,64]{0,2,1:T(8,128)(2,1)}, u32[]{:S(2)}) copy-start(bf16[2560,3,64]{0,2,1:T(8,128)(2,1)} %get-tuple-element.517) | copy-start | bytes 2949124 | tf_op jit(solution)/shard_map/while
  848.7 88.9 %reduce-scatter.13.cloned.1.call-start = ((), (), s32[]{:S(2)}) async-start(), calls=%async_computation.13 | async-start | bytes 4915200 | tf_op jit(solution)/shard_map/reduce_scatter | solution.py:174
  859.8 150.8 %reduce-scatter.21.cloned.1.call-start = ((), (), s32[]{:S(2)}) async-start(), calls=%async_computation.19 | async-start | bytes 2654208 | tf_op jit(solution)/shard_map/reduce_scatter | solution.py:216
  868.0 215.8 %reduce-scatter.23.cloned.1.call-start = ((), (), s32[]{:S(2)}) async-start(), calls=%async_computation.20 | async-start | bytes 2654208 | tf_op jit(solution)/shard_map/reduce_scatter | solution.py:217
  877.8 279.1 %reduce-scatter.19.cloned.1.call-start = ((), (), s32[]{:S(2)}) async-start(), calls=%async_computation.18 | async-start | bytes 2654208 | tf_op jit(solution)/shard_map/reduce_scatter | solution.py:214
  877.9 13.7 %copy-start.2 = (bf16[640,768]{1,0:T(8,128)(2,1)S(1)}, bf16[640,768]{1,0:T(8,128)(2,1)}, u32[]{:S(2)}) copy-start(bf16[640,768]{1,0:T(8,128)(2,1)} %param.15) | copy-start | bytes 2949124
  877.9 13.7 %copy-start.20 = (f32[640]{0:T(1024)S(1)}, f32[640]{0:T(1024)}, u32[]{:S(2)}) copy-start(f32[640]{0:T(1024)} %copy-done.19) | copy-start | bytes 7684
  877.9 13.7 %copy-start.26 = (f32[768]{0:T(1024)S(1)}, f32[768]{0:T(1024)}, u32[]{:S(2)}) copy-start(f32[768]{0:T(1024)} %copy-done.25) | copy-start | bytes 9220
  877.9 13.7 %copy-start.28 = (f32[640]{0:T(1024)S(1)}, f32[640]{0:T(1024)}, u32[]{:S(2)}) copy-start(f32[640]{0:T(1024)} %copy-done.27) | copy-start | bytes 7684
  885.7 51.9 %copy-start.6 = (bf16[640,768]{1,0:T(8,128)(2,1)S(1)}, bf16[640,768]{1,0:T(8,128)(2,1)}, u32[]{:S(2)}) copy-start(bf16[640,768]{1,0:T(8,128)(2,1)} %reduce-scatter.11.cloned.1.call-done) | copy-start | bytes 2949124
  885.7 51.9 %copy-start.7 = (bf16[640,768]{1,0:T(8,128)(2,1)S(1)}, bf16[640,768]{1,0:T(8,128)(2,1)}, u32[]{:S(2)}) copy-start(bf16[640,768]{1,0:T(8,128)(2,1)} %param.16) | copy-start | bytes 2949124
  885.7 51.9 %copy-start.18 = (f32[640]{0:T(1024)S(1)}, f32[640]{0:T(1024)}, u32[]{:S(2)}) copy-start(f32[640]{0:T(1024)} %copy-done.17) | copy-start | bytes 7684
  885.7 51.9 %copy-start.22 = (f32[768]{0:T(1024)S(1)}, f32[768]{0:T(1024)}, u32[]{:S(2)}) copy-start(f32[768]{0:T(1024)} %copy-done.21) | copy-start | bytes 9220
  885.7 51.9 %copy-start.24 = (f32[640]{0:T(1024)S(1)}, f32[640]{0:T(1024)}, u32[]{:S(2)}) copy-start(f32[640]{0:T(1024)} %copy-done.23) | copy-start | bytes 7684
  885.7 51.9 %copy-start.31 = (f32[640]{0:T(1024)S(1)}, f32[640]{0:T(1024)}, u32[]{:S(2)}) copy-start(f32[640]{0:T(1024)} %copy-done.30) | copy-start | bytes 7684
  885.7 51.9 %copy-start.33 = (f32[640]{0:T(1024)S(1)}, f32[640]{0:T(1024)}, u32[]{:S(2)}) copy-start(f32[640]{0:T(1024)} %copy-done.32) | copy-start | bytes 7684
  (24 other events, 73.9 us)
Sparse Core Ops, SparseCore 0:
  43.1 30.2 all-gather.6
  247.1 42.4 reduce-scatter.10
  420.6 42.8 reduce-scatter.14
Sparse Core Ops, SparseCore 1:
  249.6 40.9 all-gather.12
  292.0 31.2 all-gather.14
  325.3 41.4 all-gather.10
  368.9 31.2 all-gather.8
  470.5 32.8 all-gather.16
  508.4 63.3 reduce-scatter.24
  848.7 42.8 reduce-scatter.16
  894.0 42.8 reduce-scatter.12
  940.8 69.8 reduce-scatter.20
  1014.7 69.0 reduce-scatter.22
  1087.7 69.1 reduce-scatter.18
where the time goes:
time: 1170 us; the launch traced here: 1160 us
  waiting for transfers between devices  433 us (37%)
  matrix products  348 us (30%)
  other arithmetic  148 us (13%)
  blocking collectives  137 us (12%)
  local copies, waits for them, and re-layouts  71.7 us (6%)
  between operations  17.7 us (2%)
    convert_element_type x5, other arithmetic, step(): score_grad = (prob * weight_grad - signed * inner).astype(jnp.bfloat16)  76.2 us
    dot_general x5, matrix products, step(): jnp.einsum('qhd,khd->hqk', grad_block, values, preferred_element_type=jnp...  75 us
    reduce_scatter x1, waiting for transfers between devices, on_device(): lax.psum_scatter(qkv_grad, 'dp', scatter_dimension=0, tiled=True)  73.1 us
    reduce_scatter x1, waiting for transfers between devices, on_device(): lax.psum_scatter(proj_grad, 'dp', scatter_dimension=1, tiled=True)  73.1 us
    dot_general x5, matrix products, step(): jnp.einsum('hqk,qhd->khd', rounded, grad_block, preferred_element_type=jn...  69.8 us
    reduce_scatter x1, waiting for transfers between devices, on_device(): lax.psum_scatter(fc_grad, 'dp', scatter_dimension=0, tiled=True)  68.8 us
    unnamed x2, blocking collectives  61 us
    dot_general x5, matrix products, one(): jnp.einsum('hqk,khd->qhd', weights, values, preferred_element_type=jnp.fl...  52.9 us
  transfers between devices with their start and end apart: 14, of which 10 were waited for; matrix products, arithmetic and copies ran while one was open for 34% of the time, Pallas kernels for 0%

commit v1 on v0

--- a/solution.py
+++ b/solution.py
@@ -5,6 +5,27 @@
 
 HEAD = 64
 PROMPT = 512
+
+
+def in_order(blocks, dim):
+    blocks = jnp.moveaxis(blocks, 0, dim)
+    shape = blocks.shape
+    return blocks.reshape(*shape[:dim], shape[dim] * shape[dim + 1], *shape[dim + 2 :])
+
+
+def collected_by_bits(x, axis):
+    devices, position = (lax.axis_size(axis), lax.axis_index(axis))
+    parts, apart = (x[None], 1)
+    while apart < devices:
+        other = lax.ppermute(parts, axis, [(i, i ^ apart) for i in range(devices)])
+        low = position & apart == 0
+        parts = jnp.concatenate([jnp.where(low, parts, other), jnp.where(low, other, parts)])
+        apart *= 2
+    return parts
+
+
+def collect(shard, axis, dim):
+    return in_order(collected_by_bits(shard, axis), dim)
 
 
 def normalize(values):
@@ -130,7 +151,7 @@
     pieces = (w_qkv, w_out, w_fc, w_proj, ln1_gain, ln1_bias, ln2_gain, ln2_bias)
     qkv_full, out_full, fc_full, proj_full, gain1, bias1, gain2, bias2 = (
         lax.all_gather(pieces[0], "dp", axis=0, tiled=True),
-        lax.all_gather(pieces[1], "dp", axis=1, tiled=True),
+        collect(pieces[1], "dp", 1),
         lax.all_gather(pieces[2], "dp", axis=0, tiled=True),
         lax.all_gather(pieces[3], "dp", axis=1, tiled=True),
         lax.all_gather(pieces[4], "dp", axis=0, tiled=True),

time: 1170 us -> 1150 us (0.983)
  blocking collectives: 137 us -> 103 us
  waiting for transfers between devices: 433 us -> 445 us
    all_gather x1 -> x0, blocking collectives: 33.6 us -> none  [on_device(): lax.all_gather(pieces[1], 'dp', axis=1, tiled=True)]
    ppermute x0 -> x3, waiting for transfers between devices: none -> 12.1 us  [collected_by_bits(): other = lax.ppermute(parts, axis, [(i, i ^ apart) for i in range(devices)])]
  transfers between devices with their start and end apart: 14 -> 17, of which waited for: 10 -> 12; matrix products, arithmetic and copies ran while one was open for 34% -> 34% of each run, Pallas kernels for 0% -> 0%
where the time goes in v1:
time: 1150 us
  waiting for transfers between devices  445 us (39%)
  matrix products  348 us (30%)
  other arithmetic  148 us (13%)
  blocking collectives  103 us (9%)
  local copies, waits for them, and re-layouts  73.3 us (6%)
  between operations  17.8 us (2%)
    convert_element_type x5, other arithmetic, step(): score_grad = (prob * weight_grad - signed * inner).astype(jnp.bfloat16)  76.2 us
    dot_general x5, matrix products, step(): jnp.einsum('qhd,khd->hqk', grad_block, values, preferred_element_type=jnp...  74.7 us
    reduce_scatter x1, waiting for transfers between devices, on_device(): lax.psum_scatter(proj_grad, 'dp', scatter_dimension=1, tiled=True)  73.2 us
    reduce_scatter x1, waiting for transfers between devices, on_device(): lax.psum_scatter(qkv_grad, 'dp', scatter_dimension=0, tiled=True)  73 us
    dot_general x5, matrix products, step(): jnp.einsum('hqk,qhd->khd', rounded, grad_block, preferred_element_type=jn...  69.8 us
    reduce_scatter x1, waiting for transfers between devices, on_device(): lax.psum_scatter(fc_grad, 'dp', scatter_dimension=0, tiled=True)  69.1 us
    unnamed x2, blocking collectives  61 us
    dot_general x5, matrix products, one(): jnp.einsum('hqk,khd->qhd', weights, values, preferred_element_type=jnp.fl...  52.9 us
  transfers between devices with their start and end apart: 17, of which 12 were waited for; matrix products, arithmetic and copies ran while one was open for 34% of the time, Pallas kernels for 0%

profile of v1, /device:TPU:0, one launch (start us, length us, event | category | flops | bytes accessed | tf_op | source)
XLA Modules:
  0.0 1145.5 jit_solution(8026071140519724623)
XLA Ops:
  13.4 23.9 %all-reduce.10 = (bf16[768]{0:T(1024)(128)(2,1)}, bf16[768]{0:T(1024)(128)(2,1)}, bf16[768]{0:T(1024)(128)(2,1)S(1)}, bf16[768]{0:T(1024)(128)(2,1)S(1)}) all-reduce(bf16[768]{0:T(1024)(128)(2,1)S(1)} %dynamic-update-slice.3, bf16[768]{0:T(1024)(128)(2,1)S(1)} %dynamic-update-slice.2, ...), channel_id=1, replica_groups=mesh['dp'=8,'tensor'=4] {'dp'}, use_global_device_ids=true, to_apply=%add.3 | all-reduce | flops 3072 | bytes 12288
  43.5 35.4 %all_gather.36 = bf16[768,3,192]{2,1,0:T(4,128)(2,1)S(1)} all-gather(bf16[96,3,192]{2,1,0:T(4,128)(2,1)S(1)} %copy.33), channel_id=1, replica_groups=mesh['dp'=8,'tensor'=4] {'dp'}, dimensions={0}, use_global_device_ids=true | all-gather | bytes 995328 | tf_op jit(solution)/shard_map/all_gather | solution.py:153
  86.8 7.5 collective-permute-done.2
  101.7 122.7 %while.29 = (s32[]{:T(128)}, bf16[5,512,3,64]{1,3,2,0:T(8,128)(2,1)S(1)}, f32[5,3,512]{2,1,0:T(4,128)S(1)}, s32[5]{0:T(128)S(1)}, bf16[2560,3,64]{0,2,1:T(8,128)...) while((s32[]{:T(128)}, ...), condition=%wide.region_7.8_spmd.clone, body=%wide.region_4.7_spmd.clone.sunk | while | flops 1086686208 | bytes 54895824 | solution.py:96
  115.7 10.6 fusion.127
  140.1 10.6 fusion.127
  159.0 5.5 fusion.126
  164.5 10.6 fusion.127
  188.9 10.6 fusion.127
  213.3 10.6 fusion.127
  231.4 39.9 %reduce-scatter.11.cloned.1.call-done = bf16[640,768]{1,0:T(8,128)(2,1)} async-done(((bf16[2560,768]{1,0:T(8,128)(2,1)}), bf16[640,768]{1,0:T(8,128)(2,1)}) %reduce-scatter.11.cloned.1.call-update) | async-done | bytes 983056 | tf_op jit(solution)/shard_map/reduce_scatter | solution.py:182
  276.2 28.8 %all-gather.15.cloned.1.call-done = bf16[2560,768]{1,0:T(8,128)(2,1)} async-done(((bf16[640,768]{1,0:T(8,128)(2,1)}), bf16[2560,768]{1,0:T(8,128)(2,1)}) %all-gather.15.cloned.1.call-update) | async-done | bytes 3932176 | tf_op jit(solution)/shard_map/all_gather | solution.py:202
  305.0 8.8 fusion.75
  313.8 34.7 %all-gather.11.cloned.1.call-done = bf16[768,768]{1,0:T(8,128)(2,1)} async-done(((bf16[96,768]{1,0:T(8,128)(2,1)}), bf16[768,768]{1,0:T(8,128)(2,1)}) %all-gather.11.cloned.1.call-update) | async-done | bytes 1179664 | tf_op jit(solution)/shard_map/all_gather | solution.py:155
  348.4 33.4 %all-gather.9.cloned.1.call-done = bf16[2560,768]{1,0:T(8,128)(2,1)} async-done(((bf16[640,768]{1,0:T(8,128)(2,1)}), bf16[2560,768]{1,0:T(8,128)(2,1)}) %all-gather.9.cloned.1.call-update) | async-done | bytes 3932176 | tf_op jit(solution)/shard_map/all_gather | solution.py:190
  381.8 13.7 %fusion.43 = (bf16[2560,768]{1,0:T(8,128)(2,1)S(1)}, f32[2560,768]{1,0:T(8,128)}) fusion(f32[2560,768]{1,0:T(8,128)} %fusion.75, bf16[2560,768]{1,0:T(8,128)(2,1)} %all-gather.9.cloned.1.call-done, bf16[768,768]{1,0:T(8,128)(2,1)} %all-gather.11.cloned.1.call-done), kind=kOutput, calls=%fused_computation.55 | convolution fusion | flops 3059220480 | bytes 24772608 | tf_op jit(solution)/shard_map/dot_general | solution.py:191
  402.4 43.0 %reduce-scatter.15.cloned.1.call-done = bf16[640,768]{1,0:T(8,128)(2,1)} async-done(((bf16[2560,768]{1,0:T(8,128)(2,1)}), bf16[640,768]{1,0:T(8,128)(2,1)}) %reduce-scatter.15.cloned.1.call-update) | async-done | bytes 983056 | tf_op jit(solution)/shard_map/reduce_scatter | solution.py:208
  451.8 32.9 %all-gather.17.cloned.1.call-done = bf16[2560,768]{1,0:T(8,128)(2,1)} async-done(((bf16[640,768]{1,0:T(8,128)(2,1)}), bf16[2560,768]{1,0:T(8,128)(2,1)}) %all-gather.17.cloned.1.call-update) | async-done | bytes 3932176 | tf_op jit(solution)/shard_map/all_gather | solution.py:215
  494.2 323.3 %while.30 = (s32[]{:T(128)}, f32[2560,3,64]{0,2,1:T(8,128)}, f32[2560,3,64]{0,2,1:T(8,128)}, bf16[5,512,3,64]{1,0,3,2:T(8,128)(2,1)}, s32[5]{0:T(128)S(1)}, /*in...) while((s32[]{:T(128)}, f32[2560,3,64]{0,2,1:T(8,128)}, ...), condition=%wide.region_17.18_spmd.clone.clone, body=%wide.region_15.17_spmd.clone.clone.sunk | while | flops 2622784512 | bytes 218457456 | solution.py:138
  501.0 12.2 %fusion.139 = f32[2560,3,64]{0,2,1:T(8,128)} fusion(f32[3,512,2560]{2,1,0:T(8,128)S(1)} %fusion.137, f32[3,512]{1,0:T(4,128)S(1)} %dynamic-slice_bitcast_fusion.2, pred[512,2560]{1,0:T(8,128)(4,1)S(1)} %or_and_fusion.5, f32[2560,3,64]{0,2,1:T(8,128)} %get-tuple-element.498, pred[]{:T(512)S(6)} %compare.3, ...), kind=kOutput, calls=%fused_computation.30.clone.1 | convolution fusion | flops 531824640 | bytes 21174276 | tf_op jit(solution)/shard_map/while/body/eval_jaxpr/hqk,qhd->khd/dot_general | solution.py:119
  513.3 14.9 %multiply_reduce_fusion.3 = (f32[3,512]{1,0:T(4,128)S(1)}, f32[3,512,2560]{2,1,0:T(8,128)}) fusion(f32[3,512,2560]{2,1,0:T(8,128)S(1)} %fusion.137, f32[3,512]{1,0:T(4,128)S(1)} %dynamic-slice_bitcast_fusion.2, pred[512,2560]{1,0:T(8,128)(4,1)S(1)} %or_and_fusion.5, bf16[2560,3,64]{0,2,1:T(8,128)(2,1)S(1)} %copy-done.12, ...), kind=kOutput, calls=%fused_computation.19.clone.1 | convolution fusion | flops 534772224 | bytes 33959940 | tf_op jit(solution)/shard_map/while/body/eval_jaxpr/qhd,khd->hqk/dot_general | solution.py:122
  528.2 15.2 %subtract_convert_fusion.2 = bf16[3,512,2560]{2,1,0:T(8,128)(2,1)S(1)} fusion(f32[3,512,2560]{2,1,0:T(8,128)} %get-tuple-element.439, f32[3,512,2560]{2,1,0:T(8,128)} %copy-done, f32[3,512]{1,0:T(4,128)S(1)} %get-tuple-element.440, f32[3,512]{1,0:T(4,128)S(1)} %dynamic-slice_bitcast_fusion.2, pred[512,2560]{1,0:T(8,128)(4,1)S(1)} %or_and_fusion.5), kind=kLoop, calls=%fused_computation.18.clone.1 | loop fusion | flops 39321600 | bytes 40644608 | tf_op jit(solution)/shard_map/while/body/eval_jaxpr/convert_element_type | solution.py:126
  548.8 8.6 dynamic_update_slice.23
  563.9 14.4 %fusion.139 = f32[2560,3,64]{0,2,1:T(8,128)} fusion(f32[3,512,2560]{2,1,0:T(8,128)S(1)} %fusion.137, f32[3,512]{1,0:T(4,128)S(1)} %dynamic-slice_bitcast_fusion.2, pred[512,2560]{1,0:T(8,128)(4,1)S(1)} %or_and_fusion.5, f32[2560,3,64]{0,2,1:T(8,128)} %get-tuple-element.498, pred[]{:T(512)S(6)} %compare.3, ...), kind=kOutput, calls=%fused_computation.30.clone.1 | convolution fusion | flops 531824640 | bytes 21174276 | tf_op jit(solution)/shard_map/while/body/eval_jaxpr/hqk,qhd->khd/dot_general | solution.py:119
  578.3 14.9 %multiply_reduce_fusion.3 = (f32[3,512]{1,0:T(4,128)S(1)}, f32[3,512,2560]{2,1,0:T(8,128)}) fusion(f32[3,512,2560]{2,1,0:T(8,128)S(1)} %fusion.137, f32[3,512]{1,0:T(4,128)S(1)} %dynamic-slice_bitcast_fusion.2, pred[512,2560]{1,0:T(8,128)(4,1)S(1)} %or_and_fusion.5, bf16[2560,3,64]{0,2,1:T(8,128)(2,1)S(1)} %copy-done.12, ...), kind=kOutput, calls=%fused_computation.19.clone.1 | convolution fusion | flops 534772224 | bytes 33959940 | tf_op jit(solution)/shard_map/while/body/eval_jaxpr/qhd,khd->hqk/dot_general | solution.py:122
  593.2 15.2 %subtract_convert_fusion.2 = bf16[3,512,2560]{2,1,0:T(8,128)(2,1)S(1)} fusion(f32[3,512,2560]{2,1,0:T(8,128)} %get-tuple-element.439, f32[3,512,2560]{2,1,0:T(8,128)} %copy-done, f32[3,512]{1,0:T(4,128)S(1)} %get-tuple-element.440, f32[3,512]{1,0:T(4,128)S(1)} %dynamic-slice_bitcast_fusion.2, pred[512,2560]{1,0:T(8,128)(4,1)S(1)} %or_and_fusion.5), kind=kLoop, calls=%fused_computation.18.clone.1 | loop fusion | flops 39321600 | bytes 40644608 | tf_op jit(solution)/shard_map/while/body/eval_jaxpr/convert_element_type | solution.py:126
  613.8 8.6 dynamic_update_slice.23
  628.8 14.4 %fusion.139 = f32[2560,3,64]{0,2,1:T(8,128)} fusion(f32[3,512,2560]{2,1,0:T(8,128)S(1)} %fusion.137, f32[3,512]{1,0:T(4,128)S(1)} %dynamic-slice_bitcast_fusion.2, pred[512,2560]{1,0:T(8,128)(4,1)S(1)} %or_and_fusion.5, f32[2560,3,64]{0,2,1:T(8,128)} %get-tuple-element.498, pred[]{:T(512)S(6)} %compare.3, ...), kind=kOutput, calls=%fused_computation.30.clone.1 | convolution fusion | flops 531824640 | bytes 21174276 | tf_op jit(solution)/shard_map/while/body/eval_jaxpr/hqk,qhd->khd/dot_general | solution.py:119
  643.2 14.9 %multiply_reduce_fusion.3 = (f32[3,512]{1,0:T(4,128)S(1)}, f32[3,512,2560]{2,1,0:T(8,128)}) fusion(f32[3,512,2560]{2,1,0:T(8,128)S(1)} %fusion.137, f32[3,512]{1,0:T(4,128)S(1)} %dynamic-slice_bitcast_fusion.2, pred[512,2560]{1,0:T(8,128)(4,1)S(1)} %or_and_fusion.5, bf16[2560,3,64]{0,2,1:T(8,128)(2,1)S(1)} %copy-done.12, ...), kind=kOutput, calls=%fused_computation.19.clone.1 | convolution fusion | flops 534772224 | bytes 33959940 | tf_op jit(solution)/shard_map/while/body/eval_jaxpr/qhd,khd->hqk/dot_general | solution.py:122
  658.2 15.2 %subtract_convert_fusion.2 = bf16[3,512,2560]{2,1,0:T(8,128)(2,1)S(1)} fusion(f32[3,512,2560]{2,1,0:T(8,128)} %get-tuple-element.439, f32[3,512,2560]{2,1,0:T(8,128)} %copy-done, f32[3,512]{1,0:T(4,128)S(1)} %get-tuple-element.440, f32[3,512]{1,0:T(4,128)S(1)} %dynamic-slice_bitcast_fusion.2, pred[512,2560]{1,0:T(8,128)(4,1)S(1)} %or_and_fusion.5), kind=kLoop, calls=%fused_computation.18.clone.1 | loop fusion | flops 39321600 | bytes 40644608 | tf_op jit(solution)/shard_map/while/body/eval_jaxpr/convert_element_type | solution.py:126
  678.8 8.6 dynamic_update_slice.23
  693.8 14.4 %fusion.139 = f32[2560,3,64]{0,2,1:T(8,128)} fusion(f32[3,512,2560]{2,1,0:T(8,128)S(1)} %fusion.137, f32[3,512]{1,0:T(4,128)S(1)} %dynamic-slice_bitcast_fusion.2, pred[512,2560]{1,0:T(8,128)(4,1)S(1)} %or_and_fusion.5, f32[2560,3,64]{0,2,1:T(8,128)} %get-tuple-element.498, pred[]{:T(512)S(6)} %compare.3, ...), kind=kOutput, calls=%fused_computation.30.clone.1 | convolution fusion | flops 531824640 | bytes 21174276 | tf_op jit(solution)/shard_map/while/body/eval_jaxpr/hqk,qhd->khd/dot_general | solution.py:119
  708.2 14.9 %multiply_reduce_fusion.3 = (f32[3,512]{1,0:T(4,128)S(1)}, f32[3,512,2560]{2,1,0:T(8,128)}) fusion(f32[3,512,2560]{2,1,0:T(8,128)S(1)} %fusion.137, f32[3,512]{1,0:T(4,128)S(1)} %dynamic-slice_bitcast_fusion.2, pred[512,2560]{1,0:T(8,128)(4,1)S(1)} %or_and_fusion.5, bf16[2560,3,64]{0,2,1:T(8,128)(2,1)S(1)} %copy-done.12, ...), kind=kOutput, calls=%fused_computation.19.clone.1 | convolution fusion | flops 534772224 | bytes 33959940 | tf_op jit(solution)/shard_map/while/body/eval_jaxpr/qhd,khd->hqk/dot_general | solution.py:122
  723.2 15.2 %subtract_convert_fusion.2 = bf16[3,512,2560]{2,1,0:T(8,128)(2,1)S(1)} fusion(f32[3,512,2560]{2,1,0:T(8,128)} %get-tuple-element.439, f32[3,512,2560]{2,1,0:T(8,128)} %copy-done, f32[3,512]{1,0:T(4,128)S(1)} %get-tuple-element.440, f32[3,512]{1,0:T(4,128)S(1)} %dynamic-slice_bitcast_fusion.2, pred[512,2560]{1,0:T(8,128)(4,1)S(1)} %or_and_fusion.5), kind=kLoop, calls=%fused_computation.18.clone.1 | loop fusion | flops 39321600 | bytes 40644608 | tf_op jit(solution)/shard_map/while/body/eval_jaxpr/convert_element_type | solution.py:126
  743.7 8.6 dynamic_update_slice.23
  758.8 14.4 %fusion.139 = f32[2560,3,64]{0,2,1:T(8,128)} fusion(f32[3,512,2560]{2,1,0:T(8,128)S(1)} %fusion.137, f32[3,512]{1,0:T(4,128)S(1)} %dynamic-slice_bitcast_fusion.2, pred[512,2560]{1,0:T(8,128)(4,1)S(1)} %or_and_fusion.5, f32[2560,3,64]{0,2,1:T(8,128)} %get-tuple-element.498, pred[]{:T(512)S(6)} %compare.3, ...), kind=kOutput, calls=%fused_computation.30.clone.1 | convolution fusion | flops 531824640 | bytes 21174276 | tf_op jit(solution)/shard_map/while/body/eval_jaxpr/hqk,qhd->khd/dot_general | solution.py:119
  773.2 14.9 %multiply_reduce_fusion.3 = (f32[3,512]{1,0:T(4,128)S(1)}, f32[3,512,2560]{2,1,0:T(8,128)}) fusion(f32[3,512,2560]{2,1,0:T(8,128)S(1)} %fusion.137, f32[3,512]{1,0:T(4,128)S(1)} %dynamic-slice_bitcast_fusion.2, pred[512,2560]{1,0:T(8,128)(4,1)S(1)} %or_and_fusion.5, bf16[2560,3,64]{0,2,1:T(8,128)(2,1)S(1)} %copy-done.12, ...), kind=kOutput, calls=%fused_computation.19.clone.1 | convolution fusion | flops 534772224 | bytes 33959940 | tf_op jit(solution)/shard_map/while/body/eval_jaxpr/qhd,khd->hqk/dot_general | solution.py:122
  788.1 15.2 %subtract_convert_fusion.2 = bf16[3,512,2560]{2,1,0:T(8,128)(2,1)S(1)} fusion(f32[3,512,2560]{2,1,0:T(8,128)} %get-tuple-element.439, f32[3,512,2560]{2,1,0:T(8,128)} %copy-done, f32[3,512]{1,0:T(4,128)S(1)} %get-tuple-element.440, f32[3,512]{1,0:T(4,128)S(1)} %dynamic-slice_bitcast_fusion.2, pred[512,2560]{1,0:T(8,128)(4,1)S(1)} %or_and_fusion.5), kind=kLoop, calls=%fused_computation.18.clone.1 | loop fusion | flops 39321600 | bytes 40644608 | tf_op jit(solution)/shard_map/while/body/eval_jaxpr/convert_element_type | solution.py:126
  808.7 8.6 dynamic_update_slice.23
  830.8 9.9 convolution_convert_fusion.1
  840.7 8.1 fusion.76
  849.1 9.6 fusion.73
  858.8 7.7 fusion.44
  874.6 37.1 %all-reduce.8 = (f32[768]{0:T(1024)S(1)}, f32[768]{0:T(1024)S(1)}, f32[768]{0:T(1024)S(1)}, f32[768]{0:T(1024)S(1)}) all-reduce(f32[768]{0:T(1024)S(1)} %get-tuple-element.224, f32[768]{0:T(1024)S(1)} %get-tuple-element.229, f32[768]{0:T(1024)S(1)} %copy-done.34, ...), channel_id=10, replica_groups=mesh['dp'=8,'tensor'=4] {'dp'}, use_global_device_ids=true, to_apply=%region_26.27.clone | all-reduce | flops 3072 | bytes 24576
  912.0 6.4 all-reduce.9
  922.6 69.1 %reduce-scatter.21.cloned.1.call-done = f32[96,768]{1,0:T(8,128)} async-done(((f32[768,768]{1,0:T(8,128)}), f32[96,768]{1,0:T(8,128)}) %reduce-scatter.21.cloned.1.call-update) | async-done | bytes 294928 | tf_op jit(solution)/shard_map/reduce_scatter | solution.py:237
  991.7 73.2 %reduce-scatter.23.cloned.1.call-done = f32[768,96]{0,1:T(8,128)} async-done(((f32[768,768]{0,1:T(8,128)}), f32[768,96]{0,1:T(8,128)}) %reduce-scatter.23.cloned.1.call-update) | async-done | bytes 294928 | tf_op jit(solution)/shard_map/reduce_scatter | solution.py:238
  1065.0 73.0 %reduce-scatter.19.cloned.1.call-done = f32[96,3,192]{2,0,1:T(8,128)} async-done(((f32[768,3,192]{2,0,1:T(8,128)}), f32[96,3,192]{2,0,1:T(8,128)}) %reduce-scatter.19.cloned.1.call-update) | async-done | bytes 221200 | tf_op jit(solution)/shard_map/reduce_scatter | solution.py:235
  (312 shorter events, 200.8 us)
Async XLA Ops:
  8.0 35.1 %copy-start.29 = (bf16[192,96]{1,0:T(8,128)(2,1)S(1)}, bf16[192,96]{1,0:T(8,128)(2,1)}, u32[]{:S(2)}) copy-start(bf16[192,96]{1,0:T(8,128)(2,1)} %param.19) | copy-start | bytes 110596
  8.0 35.2 %copy-start.16 = (bf16[96,3,192]{2,0,1:T(8,128)(2,1)S(1)}, bf16[96,3,192]{2,0,1:T(8,128)(2,1)}, u32[]{:S(2)}) copy-start(bf16[96,3,192]{2,0,1:T(8,128)(2,1)} %param.18) | copy-start | bytes 331780
  8.0 35.3 %copy-start.40 = (s32[1,8]{1,0:T(1,128)S(1)}, s32[1,8]{1,0:T(1,128)}, u32[]{:S(2)}) copy-start(s32[1,8]{1,0:T(1,128)} %param.17) | copy-start | bytes 100
  8.0 87.7 %all-gather.7.cloned.1.call-start = ((), (), s32[]{:S(2)}) async-start(), calls=%async_computation.8 | async-start | bytes 4915200 | tf_op jit(solution)/shard_map/all_gather | solution.py:174
  43.0 228.2 %reduce-scatter.11.cloned.1.call-start = ((), (), s32[]{:S(2)}) async-start(), calls=%async_computation.9 | async-start | bytes 4915200 | tf_op jit(solution)/shard_map/reduce_scatter | solution.py:182
  43.1 37.9 %collective-permute-start = (bf16[1,192,96]{2,1,0:T(8,128)(2,1)S(1)}, bf16[1,192,96]{2,1,0:T(8,128)(2,1)S(1)}, u32[]{:S(2)}, u32[]{:S(2)}) collective-permute-start(bf16[1,192,96]{2,1,0:T(8,128)(2,1)S(1)} %bitcast.132), channel_id=1, source_target_pairs={{0,4},{4,0},{8,12},{12,8},{16,20},{20,16},{24,28},{28,24},{1,5},{5... | collective-permute-start | bytes 110600 | tf_op jit(solution)/shard_map/ppermute | solution.py:20
  81.0 14.7 %copy-start.14 = (bf16[768,3,192]{0,2,1:T(8,128)(2,1)S(1)}, bf16[768,3,192]{0,2,1:T(8,128)(2,1)}, u32[]{:S(2)}) copy-start(bf16[768,3,192]{0,2,1:T(8,128)(2,1)} %copy.34) | copy-start | bytes 2654212
  81.1 5.1 collective-permute-start.1
  86.2 8.0 collective-permute-start.2
  229.5 41.7 %copy-start.1 = (bf16[640,768]{1,0:T(8,128)(2,1)S(1)}, bf16[640,768]{1,0:T(8,128)(2,1)}, u32[]{:S(2)}) copy-start(bf16[640,768]{1,0:T(8,128)(2,1)} %param.15) | copy-start | bytes 2949124
  229.6 46.6 %all-gather.13.cloned.1.call-start = ((), (), s32[]{:S(2)}) async-start(), calls=%async_computation.12 | async-start | bytes 1327104 | tf_op jit(solution)/shard_map/all_gather | solution.py:156
  230.1 74.8 %all-gather.15.cloned.1.call-start = ((), (), s32[]{:S(2)}) async-start(), calls=%async_computation.14 | async-start | bytes 4915200 | tf_op jit(solution)/shard_map/all_gather | solution.py:202
  230.7 117.7 %all-gather.11.cloned.1.call-start = ((), (), s32[]{:S(2)}) async-start(), calls=%async_computation.11 | async-start | bytes 1327104 | tf_op jit(solution)/shard_map/all_gather | solution.py:155
  231.3 150.5 %all-gather.9.cloned.1.call-start = ((), (), s32[]{:S(2)}) async-start(), calls=%async_computation.10 | async-start | bytes 4915200 | tf_op jit(solution)/shard_map/all_gather | solution.py:190
  231.4 216.9 %copy-start.21 = (f32[768]{0:T(1024)}, f32[768]{0:T(1024)S(1)}, u32[]{:S(2)}) copy-start(f32[768]{0:T(1024)S(1)} %convert_element_type.109) | copy-start | bytes 9220
  272.9 175.4 %copy-start.17 = (f32[640]{0:T(1024)}, f32[640]{0:T(1024)S(1)}, u32[]{:S(2)}) copy-start(f32[640]{0:T(1024)S(1)} %broadcast_multiply_fusion.4) | copy-start | bytes 7684
  274.6 173.7 %copy-start.23 = (f32[640]{0:T(1024)}, f32[640]{0:T(1024)S(1)}, u32[]{:S(2)}) copy-start(f32[640]{0:T(1024)S(1)} %add_rsqrt_fusion) | copy-start | bytes 7684
  276.1 169.3 %reduce-scatter.15.cloned.1.call-start = ((), (), s32[]{:S(2)}) async-start(), calls=%async_computation.15 | async-start | bytes 4915200 | tf_op jit(solution)/shard_map/reduce_scatter | solution.py:208
  381.8 15.7 %copy-start.39 = (bf16[768,768]{1,0:T(8,128)(2,1)S(1)}, bf16[768,768]{1,0:T(8,128)(2,1)}, u32[]{:S(2)}) copy-start(bf16[768,768]{1,0:T(8,128)(2,1)} %all-gather.11.cloned.1.call-done) | copy-start | bytes 3538948
  402.4 82.3 %all-gather.17.cloned.1.call-start = ((), (), s32[]{:S(2)}) async-start(), calls=%async_computation.16 | async-start | bytes 4915200 | tf_op jit(solution)/shard_map/all_gather | solution.py:215
  448.3 41.3 %copy-start.30 = (f32[640]{0:T(1024)}, f32[640]{0:T(1024)S(1)}, u32[]{:S(2)}) copy-start(f32[640]{0:T(1024)S(1)} %get-tuple-element.303) | copy-start | bytes 7684
  448.3 41.3 %copy-start.32 = (f32[640]{0:T(1024)}, f32[640]{0:T(1024)S(1)}, u32[]{:S(2)}) copy-start(f32[640]{0:T(1024)S(1)} %get-tuple-element.304) | copy-start | bytes 7684
  451.7 415.7 %reduce-scatter.25.cloned.1.call-start = ((), (), s32[]{:S(2)}) async-start(), calls=%async_computation.21 | async-start | bytes 884736
  489.7 382.7 %reduce-scatter.17.cloned.1.call-start = ((), (), s32[]{:S(2)}) async-start(), calls=%async_computation.17 | async-start | bytes 4915200 | tf_op jit(solution)/shard_map/reduce_scatter | solution.py:228
  501.0 12.3 %copy-start = (f32[3,512,2560]{2,1,0:T(8,128)}, f32[3,512,2560]{2,1,0:T(8,128)S(1)}, u32[]{:S(2)}) copy-start(f32[3,512,2560]{2,1,0:T(8,128)S(1)} %fusion.137) | copy-start | bytes 47185924 | tf_op jit(solution)/shard_map/while
  563.8 14.4 %copy-start = (f32[3,512,2560]{2,1,0:T(8,128)}, f32[3,512,2560]{2,1,0:T(8,128)S(1)}, u32[]{:S(2)}) copy-start(f32[3,512,2560]{2,1,0:T(8,128)S(1)} %fusion.137) | copy-start | bytes 47185924 | tf_op jit(solution)/shard_map/while
  563.9 14.4 %copy-start.12 = (bf16[2560,3,64]{0,2,1:T(8,128)(2,1)S(1)}, bf16[2560,3,64]{0,2,1:T(8,128)(2,1)}, u32[]{:S(2)}) copy-start(bf16[2560,3,64]{0,2,1:T(8,128)(2,1)} %get-tuple-element.523) | copy-start | bytes 2949124 | tf_op jit(solution)/shard_map/while
  628.8 14.4 %copy-start = (f32[3,512,2560]{2,1,0:T(8,128)}, f32[3,512,2560]{2,1,0:T(8,128)S(1)}, u32[]{:S(2)}) copy-start(f32[3,512,2560]{2,1,0:T(8,128)S(1)} %fusion.137) | copy-start | bytes 47185924 | tf_op jit(solution)/shard_map/while
  628.8 14.4 %copy-start.12 = (bf16[2560,3,64]{0,2,1:T(8,128)(2,1)S(1)}, bf16[2560,3,64]{0,2,1:T(8,128)(2,1)}, u32[]{:S(2)}) copy-start(bf16[2560,3,64]{0,2,1:T(8,128)(2,1)} %get-tuple-element.523) | copy-start | bytes 2949124 | tf_op jit(solution)/shard_map/while
  693.8 14.4 %copy-start = (f32[3,512,2560]{2,1,0:T(8,128)}, f32[3,512,2560]{2,1,0:T(8,128)S(1)}, u32[]{:S(2)}) copy-start(f32[3,512,2560]{2,1,0:T(8,128)S(1)} %fusion.137) | copy-start | bytes 47185924 | tf_op jit(solution)/shard_map/while
  693.8 14.4 %copy-start.12 = (bf16[2560,3,64]{0,2,1:T(8,128)(2,1)S(1)}, bf16[2560,3,64]{0,2,1:T(8,128)(2,1)}, u32[]{:S(2)}) copy-start(bf16[2560,3,64]{0,2,1:T(8,128)(2,1)} %get-tuple-element.523) | copy-start | bytes 2949124 | tf_op jit(solution)/shard_map/while
  758.8 14.4 %copy-start = (f32[3,512,2560]{2,1,0:T(8,128)}, f32[3,512,2560]{2,1,0:T(8,128)S(1)}, u32[]{:S(2)}) copy-start(f32[3,512,2560]{2,1,0:T(8,128)S(1)} %fusion.137) | copy-start | bytes 47185924 | tf_op jit(solution)/shard_map/while
  758.8 14.4 %copy-start.12 = (bf16[2560,3,64]{0,2,1:T(8,128)(2,1)S(1)}, bf16[2560,3,64]{0,2,1:T(8,128)(2,1)}, u32[]{:S(2)}) copy-start(bf16[2560,3,64]{0,2,1:T(8,128)(2,1)} %get-tuple-element.523) | copy-start | bytes 2949124 | tf_op jit(solution)/shard_map/while
  829.5 88.9 %reduce-scatter.13.cloned.1.call-start = ((), (), s32[]{:S(2)}) async-start(), calls=%async_computation.13 | async-start | bytes 4915200 | tf_op jit(solution)/shard_map/reduce_scatter | solution.py:195
  840.7 151.0 %reduce-scatter.21.cloned.1.call-start = ((), (), s32[]{:S(2)}) async-start(), calls=%async_computation.19 | async-start | bytes 2654208 | tf_op jit(solution)/shard_map/reduce_scatter | solution.py:237
  848.9 216.1 %reduce-scatter.23.cloned.1.call-start = ((), (), s32[]{:S(2)}) async-start(), calls=%async_computation.20 | async-start | bytes 2654208 | tf_op jit(solution)/shard_map/reduce_scatter | solution.py:238
  858.8 279.2 %reduce-scatter.19.cloned.1.call-start = ((), (), s32[]{:S(2)}) async-start(), calls=%async_computation.18 | async-start | bytes 2654208 | tf_op jit(solution)/shard_map/reduce_scatter | solution.py:235
  858.8 13.6 %copy-start.2 = (bf16[640,768]{1,0:T(8,128)(2,1)S(1)}, bf16[640,768]{1,0:T(8,128)(2,1)}, u32[]{:S(2)}) copy-start(bf16[640,768]{1,0:T(8,128)(2,1)} %param.15) | copy-start | bytes 2949124
  858.8 13.6 %copy-start.20 = (f32[640]{0:T(1024)S(1)}, f32[640]{0:T(1024)}, u32[]{:S(2)}) copy-start(f32[640]{0:T(1024)} %copy-done.19) | copy-start | bytes 7684
  858.8 13.6 %copy-start.26 = (f32[768]{0:T(1024)S(1)}, f32[768]{0:T(1024)}, u32[]{:S(2)}) copy-start(f32[768]{0:T(1024)} %copy-done.25) | copy-start | bytes 9220
  858.8 13.6 %copy-start.28 = (f32[640]{0:T(1024)S(1)}, f32[640]{0:T(1024)}, u32[]{:S(2)}) copy-start(f32[640]{0:T(1024)} %copy-done.27) | copy-start | bytes 7684
  866.6 51.8 %copy-start.6 = (bf16[640,768]{1,0:T(8,128)(2,1)S(1)}, bf16[640,768]{1,0:T(8,128)(2,1)}, u32[]{:S(2)}) copy-start(bf16[640,768]{1,0:T(8,128)(2,1)} %reduce-scatter.11.cloned.1.call-done) | copy-start | bytes 2949124
  866.6 51.8 %copy-start.7 = (bf16[640,768]{1,0:T(8,128)(2,1)S(1)}, bf16[640,768]{1,0:T(8,128)(2,1)}, u32[]{:S(2)}) copy-start(bf16[640,768]{1,0:T(8,128)(2,1)} %param.16) | copy-start | bytes 2949124
  866.6 51.8 %copy-start.18 = (f32[640]{0:T(1024)S(1)}, f32[640]{0:T(1024)}, u32[]{:S(2)}) copy-start(f32[640]{0:T(1024)} %copy-done.17) | copy-start | bytes 7684
  866.6 51.8 %copy-start.22 = (f32[768]{0:T(1024)S(1)}, f32[768]{0:T(1024)}, u32[]{:S(2)}) copy-start(f32[768]{0:T(1024)} %copy-done.21) | copy-start | bytes 9220
  866.6 51.8 %copy-start.24 = (f32[640]{0:T(1024)S(1)}, f32[640]{0:T(1024)}, u32[]{:S(2)}) copy-start(f32[640]{0:T(1024)} %copy-done.23) | copy-start | bytes 7684
  866.6 51.8 %copy-start.31 = (f32[640]{0:T(1024)S(1)}, f32[640]{0:T(1024)}, u32[]{:S(2)}) copy-start(f32[640]{0:T(1024)} %copy-done.30) | copy-start | bytes 7684
  866.6 51.8 %copy-start.33 = (f32[640]{0:T(1024)S(1)}, f32[640]{0:T(1024)}, u32[]{:S(2)}) copy-start(f32[640]{0:T(1024)} %copy-done.32) | copy-start | bytes 7684
  (27 other events, 120.0 us)
Sparse Core Ops, SparseCore 0:
  43.2 30.2 all-gather.6
  229.7 41.5 reduce-scatter.10
  402.5 42.9 reduce-scatter.14
Sparse Core Ops, SparseCore 1:
  232.2 40.0 all-gather.12
  273.7 31.2 all-gather.14
  307.0 41.4 all-gather.10
  350.6 31.2 all-gather.8
  451.8 32.8 all-gather.16
  489.7 63.3 reduce-scatter.24
  829.6 42.7 reduce-scatter.16
  874.8 42.8 reduce-scatter.12
  921.6 70.1 reduce-scatter.20
  995.8 69.1 reduce-scatter.22
  1068.9 69.0 reduce-scatter.18
